TPU v7x, 32 devices: a whole 2x2x4 slice. The times are simulated.
32 devices in a mesh: gx: 4 (over y, core), gy: 8 (over z, x).
Axes of the slice: x: 2, y: 2, z: 4, core: 2. Of those that a mesh axis runs over, the one named last changes fastest.
Arguments:
- source: float32 [64, 16, 1024], P(None, 'gx', 'gy'), may hold values from -6 to 6
- initial: float32 [64, 16, 1024], P(None, 'gx', 'gy'), may hold values from -6 to 6
- reaction: float32 [64, 16, 1024], P(None, 'gx', 'gy'), may hold values from 1 to 3
- stiffness: float32 [16, 1024], P('gx', 'gy'), may hold values from 0.5 to 2
- line_op: float32 [8, 8], replicated, may hold values from -1.6 to 5.6
- face_deriv: float32 [8], replicated, may hold values from -2 to 2
- wall_flags: int32 [4, 16, 1024], P(None, 'gx', 'gy'), may hold values 0 or 1
Outputs:
- hessenberg: float32 [6, 5], replicated
- krylov_basis: float32 [6, 64, 16, 1024], P(None, None, 'gx', 'gy')
All inputs are finite; a program needn't handle non-finite values. No bound on the sum of `wall_flags` on one device may be relied on, other than what follows from the above.
Results may differ from a plain program's by a relative error of at most 0.0003.
Values sent between devices are 32-bit elements; how exact they have to be, the bound alone decides.
A program may use at most 64 MiB of HBM per device.

v0:
```python
import jax
import jax.numpy as jnp
from jax import lax
from jax.sharding import PartitionSpec as P

P_SIZE = 8
ITERS = 5


TAU = 2.0
FLOOR = 0.1


def extended(array, sides, width):
    for axis, dim in sides:
        devices, length = (lax.axis_size(axis), array.shape[dim])
        up = [(i, (i + 1) % devices) for i in range(devices)]
        down = [(j, i) for i, j in up]
        last = lax.slice_in_dim(array, length - width, length, axis=dim)
        leading = lax.slice_in_dim(array, 0, width, axis=dim)
        before = lax.ppermute(last, axis, up)
        after = lax.ppermute(leading, axis, down)
        array = jnp.concatenate([before, array, after], axis=dim)
    return array


def local_total(values):
    return jnp.sum(jnp.sum(values, axis=0))


def x_traces(nodes, face_deriv):
    highest = lax.Precision.HIGHEST
    lower = jnp.einsum("c,cbxy->bxy", face_deriv, nodes, precision=highest)
    upper = jnp.einsum("c,cbxy->bxy", face_deriv[::-1], nodes, precision=highest)
    return jnp.stack([nodes[0], lower, nodes[-1], upper])


def y_traces(nodes, face_deriv):
    highest = lax.Precision.HIGHEST
    lower = jnp.einsum("c,acxy->axy", face_deriv, nodes, precision=highest)
    upper = jnp.einsum("c,acxy->axy", face_deriv[::-1], nodes, precision=highest)
    return jnp.stack([nodes[:, 0], lower, nodes[:, -1], upper])


def apply_op(field, reaction, stiffness, line_op, face_deriv, opened):
    highest = lax.Precision.HIGHEST
    nodes = field.reshape(P_SIZE, P_SIZE, field.shape[1], field.shape[2])
    interior = stiffness * (
        jnp.einsum("ac,cbxy->abxy", line_op, nodes, precision=highest)
        + jnp.einsum("bc,acxy->abxy", line_op, nodes, precision=highest)
    )
    padded = extended(nodes, (("gx", 2), ("gy", 3)), 1)
    xside = x_traces(padded, face_deriv)[:, :, :, 1:-1]
    yside = y_traces(padded, face_deriv)[:, :, 1:-1, :]
    x_own = xside[:, :, 1:-1]
    y_own = yside[:, :, :, 1:-1]
    east_nb = xside[0:2, :, 2:]
    west_nb = xside[2:4, :, :-2]
    north_nb = yside[0:2, :, :, 2:]
    south_nb = yside[2:4, :, :, :-2]
    add_east = TAU * (x_own[2] - opened[1] * east_nb[0]) + 0.5 * (x_own[3] - opened[1] * east_nb[1])
    add_west = TAU * (x_own[0] - opened[0] * west_nb[0]) + 0.5 * (x_own[1] - opened[0] * west_nb[1])
    add_north = TAU * (y_own[2] - opened[3] * north_nb[0]) + 0.5 * (
        y_own[3] - opened[3] * north_nb[1]
    )
    add_south = TAU * (y_own[0] - opened[2] * south_nb[0]) + 0.5 * (
        y_own[1] - opened[2] * south_nb[1]
    )
    result = reaction.reshape(nodes.shape) * nodes + interior
    result = result.at[0].add(add_west).at[P_SIZE - 1].add(add_east)
    result = result.at[:, 0].add(add_south).at[:, P_SIZE - 1].add(add_north)
    return result.reshape(field.shape)


def norm_scale(vector, total):
    squares = lax.psum(local_total(vector * vector), ("gx", "gy"))
    return jnp.sqrt(squares / total + FLOOR)


def body(source, initial, reaction, stiffness, line_op, face_deriv, wall_flags):
    highest = lax.Precision.HIGHEST
    total = float(
        P_SIZE
        * P_SIZE
        * source.shape[1]
        * lax.axis_size("gx")
        * source.shape[2]
        * lax.axis_size("gy")
    )
    opened = 1.0 - wall_flags.astype(jnp.float32)

    def operate(field):
        return apply_op(field, reaction, stiffness, line_op, face_deriv, opened)

    def products(basis, image):
        per_cell = jnp.einsum("kqxy,qxy->kxy", basis, image, precision=highest)
        return jnp.sum(per_cell, axis=(1, 2))

    first = source - operate(initial)
    basis = jnp.zeros((ITERS + 1,) + source.shape, jnp.float32)
    hessen = jnp.zeros((ITERS + 1, ITERS), jnp.float32)
    rows = lax.broadcasted_iota(jnp.int32, (ITERS + 1, ITERS), 0)
    cols = lax.broadcasted_iota(jnp.int32, (ITERS + 1, ITERS), 1)
    slots = lax.broadcasted_iota(jnp.int32, (ITERS + 1,), 0)

    def advance(step, carry):
        basis, hessen, pending = carry
        image = operate(pending)
        local = products(basis, image)
        projected, crossed, squares = lax.psum(
            (local, local_total(pending * image), local_total(pending * pending)), ("gx", "gy")
        )
        beta = jnp.sqrt(squares / total + FLOOR)
        basis = lax.dynamic_update_index_in_dim(basis, pending / beta, step, 0)
        coeffs = projected / (total * beta) + jnp.where(
            slots == step, crossed / (total * beta * beta), 0.0
        )
        pending = image / beta - jnp.einsum("k,kqxy->qxy", coeffs, basis, precision=highest)
        hessen = hessen + jnp.where(cols == step, coeffs[:, None], 0.0)
        hessen = hessen + jnp.where((rows == step) & (cols == step - 1), beta, 0.0)
        return (basis, hessen, pending)

    basis, hessen, pending = lax.fori_loop(0, ITERS, advance, (basis, hessen, first))
    beta = norm_scale(pending, total)
    basis = basis.at[ITERS].set(pending / beta)
    hessen = hessen + jnp.where((rows == ITERS) & (cols == ITERS - 1), beta, 0.0)
    return (hessen, basis)


def solution(mesh):
    return jax.shard_map(
        body,
        mesh=mesh,
        in_specs=(
            P(None, "gx", "gy"),
            P(None, "gx", "gy"),
            P(None, "gx", "gy"),
            P("gx", "gy"),
            P(),
            P(),
            P(None, "gx", "gy"),
        ),
        out_specs=(P(), P(None, None, "gx", "gy")),
        check_vma=False,
    )
```

profile of v0, /device:TPU:0, one launch (start us, length us, event | category | flops | bytes accessed | tf_op | source)
XLA Modules:
  0.0 408.1 jit_solution(16767970016116543631)
XLA Ops:
  2.2 2.0 collective-permute-start.5
  6.0 2.2 collective-permute-start.6
  8.2 3.1 collective-permute-start.7
  12.3 4.8 %collective-permute-done.6 = f32[8,8,6,1]{3,0,2,1:T(8,128)S(1)} collective-permute-done((f32[8,8,6,1]{3,0,2,1:T(8,128)S(1)}, f32[8,8,6,1]{3,0,2,1:T(8,128)S(1)}, u32[]{:S(2)}, u32[]{:S(2)}) %collective-permute-start.6) | collective-permute-done | bytes 1568 | tf_op jit(solution)/shard_map/ppermute | solution.py:21
  17.1 2.8 collective-permute-done.7
  26.0 339.5 %while.31 = (s32[]{:T(128)}, f32[6,64,4,128]{3,2,1,0:T(4,128)S(1)}, f32[6,5]{1,0:T(8,128)S(1)}, f32[64,4,128]{2,1,0:T(4,128)S(1)}, f32[64,4,128]{2,0,1:T(8,128)S...) while((s32[]{:T(128)}, f32[6,64,4,128]{3,2,1,0:T(4,128)S(1)}, ...), condition=%wide.region_6.7_spmd.clone.clone, body=%wide.region_0.6_spmd.clone.clone.sunk | while | flops 14006069 | bytes 9489035 | solution.py:123
  29.6 2.8 collective-permute-start.2
  32.7 4.3 %collective-permute-done.2 = f32[8,8,6,1]{3,0,2,1:T(8,128)S(1)} collective-permute-done((f32[8,8,6,1]{3,0,2,1:T(8,128)S(1)}, f32[8,8,6,1]{3,0,2,1:T(8,128)S(1)}, u32[]{:S(2)}, u32[]{:S(2)}) %collective-permute-start.2) | collective-permute-done | bytes 1568 | tf_op jit(solution)/shard_map/while/body/eval_jaxpr/ppermute | solution.py:22
  37.0 5.2 %collective-permute-done.3 = f32[8,8,6,1]{3,0,2,1:T(8,128)S(1)} collective-permute-done((f32[8,8,6,1]{3,0,2,1:T(8,128)S(1)}, f32[8,8,6,1]{3,0,2,1:T(8,128)S(1)}, u32[]{:S(2)}, u32[]{:S(2)}) %collective-permute-start.3) | collective-permute-done | bytes 1568 | tf_op jit(solution)/shard_map/while/body/eval_jaxpr/ppermute | solution.py:21
  47.3 2.6 convolution_bitcast_fusion.2
  49.8 39.4 %all-reduce.2 = (f32[]{:T(128)}, f32[6]{0:T(128)S(1)}, f32[]{:T(128)}) all-reduce(f32[]{:T(128)} %get-tuple-element.835, f32[6]{0:T(128)S(1)} %convolution_bitcast_fusion.2, f32[]{:T(128)} %fusion.189), channel_id=1, replica_groups=mesh['gx'=4,'gy'=8] {'gx','gy'}, use_global_device_ids=true, to_apply=%region_2.2 | all-reduce | flops 8 | bytes 64 | tf_op jit(solution)/shard_map/while/body/eval_jaxpr/psum | solution.py:110
  96.8 3.9 collective-permute-start.2
  101.0 4.9 %collective-permute-done.2 = f32[8,8,6,1]{3,0,2,1:T(8,128)S(1)} collective-permute-done((f32[8,8,6,1]{3,0,2,1:T(8,128)S(1)}, f32[8,8,6,1]{3,0,2,1:T(8,128)S(1)}, u32[]{:S(2)}, u32[]{:S(2)}) %collective-permute-start.2) | collective-permute-done | bytes 1568 | tf_op jit(solution)/shard_map/while/body/eval_jaxpr/ppermute | solution.py:22
  105.9 5.1 %collective-permute-done.3 = f32[8,8,6,1]{3,0,2,1:T(8,128)S(1)} collective-permute-done((f32[8,8,6,1]{3,0,2,1:T(8,128)S(1)}, f32[8,8,6,1]{3,0,2,1:T(8,128)S(1)}, u32[]{:S(2)}, u32[]{:S(2)}) %collective-permute-start.3) | collective-permute-done | bytes 1568 | tf_op jit(solution)/shard_map/while/body/eval_jaxpr/ppermute | solution.py:21
  116.0 2.6 convolution_bitcast_fusion.2
  118.6 39.2 %all-reduce.2 = (f32[]{:T(128)}, f32[6]{0:T(128)S(1)}, f32[]{:T(128)}) all-reduce(f32[]{:T(128)} %get-tuple-element.835, f32[6]{0:T(128)S(1)} %convolution_bitcast_fusion.2, f32[]{:T(128)} %fusion.189), channel_id=1, replica_groups=mesh['gx'=4,'gy'=8] {'gx','gy'}, use_global_device_ids=true, to_apply=%region_2.2 | all-reduce | flops 8 | bytes 64 | tf_op jit(solution)/shard_map/while/body/eval_jaxpr/psum | solution.py:110
  165.4 3.9 collective-permute-start.2
  169.6 4.6 %collective-permute-done.2 = f32[8,8,6,1]{3,0,2,1:T(8,128)S(1)} collective-permute-done((f32[8,8,6,1]{3,0,2,1:T(8,128)S(1)}, f32[8,8,6,1]{3,0,2,1:T(8,128)S(1)}, u32[]{:S(2)}, u32[]{:S(2)}) %collective-permute-start.2) | collective-permute-done | bytes 1568 | tf_op jit(solution)/shard_map/while/body/eval_jaxpr/ppermute | solution.py:22
  174.2 4.9 %collective-permute-done.3 = f32[8,8,6,1]{3,0,2,1:T(8,128)S(1)} collective-permute-done((f32[8,8,6,1]{3,0,2,1:T(8,128)S(1)}, f32[8,8,6,1]{3,0,2,1:T(8,128)S(1)}, u32[]{:S(2)}, u32[]{:S(2)}) %collective-permute-start.3) | collective-permute-done | bytes 1568 | tf_op jit(solution)/shard_map/while/body/eval_jaxpr/ppermute | solution.py:21
  184.1 2.6 convolution_bitcast_fusion.2
  186.7 39.1 %all-reduce.2 = (f32[]{:T(128)}, f32[6]{0:T(128)S(1)}, f32[]{:T(128)}) all-reduce(f32[]{:T(128)} %get-tuple-element.835, f32[6]{0:T(128)S(1)} %convolution_bitcast_fusion.2, f32[]{:T(128)} %fusion.189), channel_id=1, replica_groups=mesh['gx'=4,'gy'=8] {'gx','gy'}, use_global_device_ids=true, to_apply=%region_2.2 | all-reduce | flops 8 | bytes 64 | tf_op jit(solution)/shard_map/while/body/eval_jaxpr/psum | solution.py:110
  233.3 3.9 collective-permute-start.2
  237.6 4.6 %collective-permute-done.2 = f32[8,8,6,1]{3,0,2,1:T(8,128)S(1)} collective-permute-done((f32[8,8,6,1]{3,0,2,1:T(8,128)S(1)}, f32[8,8,6,1]{3,0,2,1:T(8,128)S(1)}, u32[]{:S(2)}, u32[]{:S(2)}) %collective-permute-start.2) | collective-permute-done | bytes 1568 | tf_op jit(solution)/shard_map/while/body/eval_jaxpr/ppermute | solution.py:22
  242.1 4.9 %collective-permute-done.3 = f32[8,8,6,1]{3,0,2,1:T(8,128)S(1)} collective-permute-done((f32[8,8,6,1]{3,0,2,1:T(8,128)S(1)}, f32[8,8,6,1]{3,0,2,1:T(8,128)S(1)}, u32[]{:S(2)}, u32[]{:S(2)}) %collective-permute-start.3) | collective-permute-done | bytes 1568 | tf_op jit(solution)/shard_map/while/body/eval_jaxpr/ppermute | solution.py:21
  252.1 2.6 convolution_bitcast_fusion.2
  254.7 39.1 %all-reduce.2 = (f32[]{:T(128)}, f32[6]{0:T(128)S(1)}, f32[]{:T(128)}) all-reduce(f32[]{:T(128)} %get-tuple-element.835, f32[6]{0:T(128)S(1)} %convolution_bitcast_fusion.2, f32[]{:T(128)} %fusion.189), channel_id=1, replica_groups=mesh['gx'=4,'gy'=8] {'gx','gy'}, use_global_device_ids=true, to_apply=%region_2.2 | all-reduce | flops 8 | bytes 64 | tf_op jit(solution)/shard_map/while/body/eval_jaxpr/psum | solution.py:110
  301.3 3.9 collective-permute-start.2
  305.5 4.6 %collective-permute-done.2 = f32[8,8,6,1]{3,0,2,1:T(8,128)S(1)} collective-permute-done((f32[8,8,6,1]{3,0,2,1:T(8,128)S(1)}, f32[8,8,6,1]{3,0,2,1:T(8,128)S(1)}, u32[]{:S(2)}, u32[]{:S(2)}) %collective-permute-start.2) | collective-permute-done | bytes 1568 | tf_op jit(solution)/shard_map/while/body/eval_jaxpr/ppermute | solution.py:22
  310.1 4.9 %collective-permute-done.3 = f32[8,8,6,1]{3,0,2,1:T(8,128)S(1)} collective-permute-done((f32[8,8,6,1]{3,0,2,1:T(8,128)S(1)}, f32[8,8,6,1]{3,0,2,1:T(8,128)S(1)}, u32[]{:S(2)}, u32[]{:S(2)}) %collective-permute-start.3) | collective-permute-done | bytes 1568 | tf_op jit(solution)/shard_map/while/body/eval_jaxpr/ppermute | solution.py:21
  320.0 2.6 convolution_bitcast_fusion.2
  322.6 39.1 %all-reduce.2 = (f32[]{:T(128)}, f32[6]{0:T(128)S(1)}, f32[]{:T(128)}) all-reduce(f32[]{:T(128)} %get-tuple-element.835, f32[6]{0:T(128)S(1)} %convolution_bitcast_fusion.2, f32[]{:T(128)} %fusion.189), channel_id=1, replica_groups=mesh['gx'=4,'gy'=8] {'gx','gy'}, use_global_device_ids=true, to_apply=%region_2.2 | all-reduce | flops 8 | bytes 64 | tf_op jit(solution)/shard_map/while/body/eval_jaxpr/psum | solution.py:110
  366.2 40.3 %psum.52 = f32[]{:T(128)} all-reduce(f32[]{:T(128)} %multiply_reduce_fusion.2), channel_id=1, replica_groups=mesh['gx'=4,'gy'=8] {'gx','gy'}, use_global_device_ids=true, to_apply=%region_8.9 | all-reduce | flops 1 | bytes 8 | tf_op jit(solution)/shard_map/psum | solution.py:76
  (322 shorter events, 68.2 us)
Async XLA Ops:
  1.5 2.6 copy-start.5
  1.6 4.1 %collective-permute-start.4 = (f32[8,8,1,128]{3,0,2,1:T(8,128)S(1)}, f32[8,8,1,128]{3,0,2,1:T(8,128)S(1)}, u32[]{:S(2)}, u32[]{:S(2)}) collective-permute-start(f32[8,8,1,128]{3,0,2,1:T(8,128)S(1)} %copy.247), channel_id=1, source_target_pairs={{0,8},{8,16},{16,24},{24,0},{1,9},{9,17},{17,25},{25,1},{2,10},{10... | collective-permute-start | bytes 98312 | tf_op jit(solution)/shard_map/ppermute | solution.py:21
  2.1 2.1 copy-start.11
  2.2 3.7 collective-permute-start.5
  5.5 6.7 %copy-start.3 = (f32[8,8,4,128]{3,0,2,1:T(8,128)}, f32[8,8,4,128]{3,0,2,1:T(8,128)S(1)}, u32[]{:S(2)}) copy-start(f32[8,8,4,128]{3,0,2,1:T(8,128)S(1)} %fusion.62) | copy-start | bytes 393220
  6.0 11.1 %collective-permute-start.6 = (f32[8,8,6,1]{3,0,2,1:T(8,128)S(1)}, f32[8,8,6,1]{3,0,2,1:T(8,128)S(1)}, u32[]{:S(2)}, u32[]{:S(2)}) collective-permute-start(f32[8,8,6,1]{3,0,2,1:T(8,128)S(1)} %get-tuple-element.682), channel_id=1, source_target_pairs={{0,1},{1,2},{2,3},{3,4},{4,5},{5,6},{6,7},{7,0},{8,9},{9,10},{10,1... | collective-permute-start | bytes 4616 | tf_op jit(solution)/shard_map/ppermute | solution.py:21
  8.2 11.6 %collective-permute-start.7 = (f32[8,8,6,1]{3,0,2,1:T(8,128)S(1)}, f32[8,8,6,1]{3,0,2,1:T(8,128)S(1)}, u32[]{:S(2)}, u32[]{:S(2)}) collective-permute-start(f32[8,8,6,1]{3,0,2,1:T(8,128)S(1)} %get-tuple-element.683), channel_id=1, source_target_pairs={{1,0},{2,1},{3,2},{4,3},{5,4},{6,5},{7,6},{0,7},{9,8},{10,9},{11,1... | collective-permute-start | bytes 4616 | tf_op jit(solution)/shard_map/ppermute | solution.py:22
  26.1 3.4 collective-permute-start
  26.3 3.2 collective-permute-start.1
  28.5 4.2 %copy-start.1 = (f32[8,8,4,128]{3,0,2,1:T(8,128)}, f32[8,8,4,128]{3,0,2,1:T(8,128)S(1)}, u32[]{:S(2)}) copy-start(f32[8,8,4,128]{3,0,2,1:T(8,128)S(1)} %fusion.175) | copy-start | bytes 393220 | tf_op jit(solution)/shard_map/while
  29.6 7.4 %collective-permute-start.2 = (f32[8,8,6,1]{3,0,2,1:T(8,128)S(1)}, f32[8,8,6,1]{3,0,2,1:T(8,128)S(1)}, u32[]{:S(2)}, u32[]{:S(2)}) collective-permute-start(f32[8,8,6,1]{3,0,2,1:T(8,128)S(1)} %get-tuple-element.788), channel_id=1, source_target_pairs={{1,0},{2,1},{3,2},{4,3},{5,4},{6,5},{7,6},{0,7},{9,8},{10,9},{11,1... | collective-permute-start | bytes 4616 | tf_op jit(solution)/shard_map/while/body/eval_jaxpr/ppermute | solution.py:22
  32.4 9.8 %collective-permute-start.3 = (f32[8,8,6,1]{3,0,2,1:T(8,128)S(1)}, f32[8,8,6,1]{3,0,2,1:T(8,128)S(1)}, u32[]{:S(2)}, u32[]{:S(2)}) collective-permute-start(f32[8,8,6,1]{3,0,2,1:T(8,128)S(1)} %get-tuple-element.789), channel_id=1, source_target_pairs={{0,1},{1,2},{2,3},{3,4},{4,5},{5,6},{6,7},{7,0},{8,9},{9,10},{10,1... | collective-permute-start | bytes 4616 | tf_op jit(solution)/shard_map/while/body/eval_jaxpr/ppermute | solution.py:21
  93.1 3.4 collective-permute-start
  93.2 3.5 collective-permute-start.1
  95.5 5.4 %copy-start.1 = (f32[8,8,4,128]{3,0,2,1:T(8,128)}, f32[8,8,4,128]{3,0,2,1:T(8,128)S(1)}, u32[]{:S(2)}) copy-start(f32[8,8,4,128]{3,0,2,1:T(8,128)S(1)} %fusion.175) | copy-start | bytes 393220 | tf_op jit(solution)/shard_map/while
  96.8 9.2 %collective-permute-start.2 = (f32[8,8,6,1]{3,0,2,1:T(8,128)S(1)}, f32[8,8,6,1]{3,0,2,1:T(8,128)S(1)}, u32[]{:S(2)}, u32[]{:S(2)}) collective-permute-start(f32[8,8,6,1]{3,0,2,1:T(8,128)S(1)} %get-tuple-element.788), channel_id=1, source_target_pairs={{1,0},{2,1},{3,2},{4,3},{5,4},{6,5},{7,6},{0,7},{9,8},{10,9},{11,1... | collective-permute-start | bytes 4616 | tf_op jit(solution)/shard_map/while/body/eval_jaxpr/ppermute | solution.py:22
  100.7 10.3 %collective-permute-start.3 = (f32[8,8,6,1]{3,0,2,1:T(8,128)S(1)}, f32[8,8,6,1]{3,0,2,1:T(8,128)S(1)}, u32[]{:S(2)}, u32[]{:S(2)}) collective-permute-start(f32[8,8,6,1]{3,0,2,1:T(8,128)S(1)} %get-tuple-element.789), channel_id=1, source_target_pairs={{0,1},{1,2},{2,3},{3,4},{4,5},{5,6},{6,7},{7,0},{8,9},{9,10},{10,1... | collective-permute-start | bytes 4616 | tf_op jit(solution)/shard_map/while/body/eval_jaxpr/ppermute | solution.py:21
  161.7 3.4 collective-permute-start
  161.8 3.5 collective-permute-start.1
  164.1 5.4 %copy-start.1 = (f32[8,8,4,128]{3,0,2,1:T(8,128)}, f32[8,8,4,128]{3,0,2,1:T(8,128)S(1)}, u32[]{:S(2)}) copy-start(f32[8,8,4,128]{3,0,2,1:T(8,128)S(1)} %fusion.175) | copy-start | bytes 393220 | tf_op jit(solution)/shard_map/while
  165.4 8.8 %collective-permute-start.2 = (f32[8,8,6,1]{3,0,2,1:T(8,128)S(1)}, f32[8,8,6,1]{3,0,2,1:T(8,128)S(1)}, u32[]{:S(2)}, u32[]{:S(2)}) collective-permute-start(f32[8,8,6,1]{3,0,2,1:T(8,128)S(1)} %get-tuple-element.788), channel_id=1, source_target_pairs={{1,0},{2,1},{3,2},{4,3},{5,4},{6,5},{7,6},{0,7},{9,8},{10,9},{11,1... | collective-permute-start | bytes 4616 | tf_op jit(solution)/shard_map/while/body/eval_jaxpr/ppermute | solution.py:22
  169.3 9.8 %collective-permute-start.3 = (f32[8,8,6,1]{3,0,2,1:T(8,128)S(1)}, f32[8,8,6,1]{3,0,2,1:T(8,128)S(1)}, u32[]{:S(2)}, u32[]{:S(2)}) collective-permute-start(f32[8,8,6,1]{3,0,2,1:T(8,128)S(1)} %get-tuple-element.789), channel_id=1, source_target_pairs={{0,1},{1,2},{2,3},{3,4},{4,5},{5,6},{6,7},{7,0},{8,9},{9,10},{10,1... | collective-permute-start | bytes 4616 | tf_op jit(solution)/shard_map/while/body/eval_jaxpr/ppermute | solution.py:21
  229.7 3.4 collective-permute-start
  229.7 3.5 collective-permute-start.1
  232.1 5.4 %copy-start.1 = (f32[8,8,4,128]{3,0,2,1:T(8,128)}, f32[8,8,4,128]{3,0,2,1:T(8,128)S(1)}, u32[]{:S(2)}) copy-start(f32[8,8,4,128]{3,0,2,1:T(8,128)S(1)} %fusion.175) | copy-start | bytes 393220 | tf_op jit(solution)/shard_map/while
  233.3 8.8 %collective-permute-start.2 = (f32[8,8,6,1]{3,0,2,1:T(8,128)S(1)}, f32[8,8,6,1]{3,0,2,1:T(8,128)S(1)}, u32[]{:S(2)}, u32[]{:S(2)}) collective-permute-start(f32[8,8,6,1]{3,0,2,1:T(8,128)S(1)} %get-tuple-element.788), channel_id=1, source_target_pairs={{1,0},{2,1},{3,2},{4,3},{5,4},{6,5},{7,6},{0,7},{9,8},{10,9},{11,1... | collective-permute-start | bytes 4616 | tf_op jit(solution)/shard_map/while/body/eval_jaxpr/ppermute | solution.py:22
  237.3 9.8 %collective-permute-start.3 = (f32[8,8,6,1]{3,0,2,1:T(8,128)S(1)}, f32[8,8,6,1]{3,0,2,1:T(8,128)S(1)}, u32[]{:S(2)}, u32[]{:S(2)}) collective-permute-start(f32[8,8,6,1]{3,0,2,1:T(8,128)S(1)} %get-tuple-element.789), channel_id=1, source_target_pairs={{0,1},{1,2},{2,3},{3,4},{4,5},{5,6},{6,7},{7,0},{8,9},{9,10},{10,1... | collective-permute-start | bytes 4616 | tf_op jit(solution)/shard_map/while/body/eval_jaxpr/ppermute | solution.py:21
  297.6 3.4 collective-permute-start
  297.7 3.5 collective-permute-start.1
  300.0 5.4 %copy-start.1 = (f32[8,8,4,128]{3,0,2,1:T(8,128)}, f32[8,8,4,128]{3,0,2,1:T(8,128)S(1)}, u32[]{:S(2)}) copy-start(f32[8,8,4,128]{3,0,2,1:T(8,128)S(1)} %fusion.175) | copy-start | bytes 393220 | tf_op jit(solution)/shard_map/while
  301.3 8.8 %collective-permute-start.2 = (f32[8,8,6,1]{3,0,2,1:T(8,128)S(1)}, f32[8,8,6,1]{3,0,2,1:T(8,128)S(1)}, u32[]{:S(2)}, u32[]{:S(2)}) collective-permute-start(f32[8,8,6,1]{3,0,2,1:T(8,128)S(1)} %get-tuple-element.788), channel_id=1, source_target_pairs={{1,0},{2,1},{3,2},{4,3},{5,4},{6,5},{7,6},{0,7},{9,8},{10,9},{11,1... | collective-permute-start | bytes 4616 | tf_op jit(solution)/shard_map/while/body/eval_jaxpr/ppermute | solution.py:22
  305.2 9.8 %collective-permute-start.3 = (f32[8,8,6,1]{3,0,2,1:T(8,128)S(1)}, f32[8,8,6,1]{3,0,2,1:T(8,128)S(1)}, u32[]{:S(2)}, u32[]{:S(2)}) collective-permute-start(f32[8,8,6,1]{3,0,2,1:T(8,128)S(1)} %get-tuple-element.789), channel_id=1, source_target_pairs={{0,1},{1,2},{2,3},{3,4},{4,5},{5,6},{6,7},{7,0},{8,9},{9,10},{10,1... | collective-permute-start | bytes 4616 | tf_op jit(solution)/shard_map/while/body/eval_jaxpr/ppermute | solution.py:21
  (18 other events, 16.1 us)
where the time goes:
time: 410 us; the launch traced here: 408 us
  blocking collectives  236 us (58%)
  waiting for transfers between devices  61.2 us (15%)
  matrix products  36.9 us (9%)
  starting transfers between devices  35.6 us (9%)
  local copies, waits for them, and re-layouts  15.6 us (4%)
  other arithmetic  13.3 us (3%)
  loops' own time  7.86 us (2%)
    psum x5, blocking collectives, advance(): lax.psum((local, local_total(pending * image), local_total(pending * pend...  196 us
    psum x1, blocking collectives, norm_scale(): squares = lax.psum(local_total(vector * vector), ('gx', 'gy'))  40.3 us
    ppermute x12, waiting for transfers between devices, extended(): before = lax.ppermute(last, axis, up)  34.7 us
    ppermute x12, starting transfers between devices, extended(): after = lax.ppermute(leading, axis, down)  32.4 us
    ppermute x12, waiting for transfers between devices, extended(): after = lax.ppermute(leading, axis, down)  26.5 us
    dot_general x5, matrix products, products(): per_cell = jnp.einsum('kqxy,qxy->kxy', basis, image, precision=highest)  13 us
    reduce_sum x12, other arithmetic, local_total(): return jnp.sum(jnp.sum(values, axis=0))  8.74 us
  transfers between devices with their start and end apart: 24, of which 23 were waited for; matrix products, arithmetic and copies ran while one was open for 1% of the time, Pallas kernels for 0%

commit v1 on v0

v1 whole, which is shorter than its diff:
```python
import functools

import jax
import jax.numpy as jnp
from jax import lax
from jax.experimental import pallas as pl
from jax.experimental.pallas import tpu as pltpu
from jax.sharding import PartitionSpec as P

P_SIZE = 8
ITERS = 5
TAU = 2.0
FLOOR = 0.1
PAIRS = P_SIZE // 2
MESH = pl.DeviceIdType.MESH


def kernel(
    nx, ny, total,
    line, deriv, src, ini, rea, stf, wal,
    hess_out, basis_out,
    pend, image, bas, coef, gcoef, small,
    hsend, hrecv, rsend, rrecv,
    hs_sem, hr_sem, rs_sem, rr_sem, out_sem,
):
    n = nx * ny
    gx, gy = lax.axis_index("gx"), lax.axis_index("gy")
    me = gx * ny + gy

    def peer(k):
        t = lax.rem(me + k, n)
        return (t // ny, lax.rem(t, ny))

    east = (lax.rem(gx + 1, nx), gy)
    west = (lax.rem(gx + nx - 1, nx), gy)
    north = (gx, lax.rem(gy + 1, ny))
    south = (gx, lax.rem(gy + ny - 1, ny))

    barrier = pltpu.get_barrier_semaphore()

    def greet(k, carry):
        pl.semaphore_signal(barrier, inc=1, device_id=peer(k), device_id_type=MESH)
        return carry

    lax.fori_loop(1, n, greet, 0, unroll=n <= 64)

    sub = lax.broadcasted_iota(jnp.int32, (8, 128), 0)
    lane = lax.broadcasted_iota(jnp.int32, (8, 128), 1)
    low = sub < 4
    xpos = sub % 4

    def srl(v, s):
        s = s % 8
        return v if s == 0 else pltpu.roll(v, s, 0)

    def lrl(v, s):
        s = s % 128
        return v if s == 0 else pltpu.roll(v, s, 1)

    def halves(a, b):
        return jnp.where(low, a, b)

    for p in range(PAIRS):
        for r in range(PAIRS):
            coef[(p * PAIRS + r) * 2] = halves(line[2 * p, 2 * r], line[2 * p + 1, 2 * r + 1])
            coef[(p * PAIRS + r) * 2 + 1] = halves(line[2 * p, 2 * r + 1], line[2 * p + 1, 2 * r])
    glow = [0.5 * deriv[c] + (TAU if c == 0 else 0.0) for c in range(P_SIZE)]
    gupp = [
        0.5 * deriv[P_SIZE - 1 - c] + (TAU if c == P_SIZE - 1 else 0.0) for c in range(P_SIZE)
    ]
    for p in range(PAIRS):
        gcoef[p] = halves(glow[2 * p], glow[2 * p + 1])
        gcoef[PAIRS + p] = halves(gupp[2 * p], gupp[2 * p + 1])
    small[0, 0:4] = stf[...]
    small[0, 4:8] = stf[...]
    opened = [1.0 - wal[f].astype(jnp.float32) for f in range(4)]
    for slot, (first, second) in enumerate(((0, 0), (1, 1), (2, 3))):
        small[slot + 1, 0:4] = opened[first]
        small[slot + 1, 4:8] = opened[second]

    def tile(ref, a, p):
        return ref[pl.ds((a * PAIRS + p) * 8, 8), :]

    def put(ref, a, p, value):
        ref[pl.ds((a * PAIRS + p) * 8, 8), :] = value

    def xfaces(get):
        fw, fe = [], []
        for p in range(PAIRS):
            w = e = None
            for c in range(P_SIZE):
                v = get(c, p)
                w = glow[c] * v if w is None else w + glow[c] * v
                e = gupp[c] * v if e is None else e + gupp[c] * v
            fw.append(w)
            fe.append(e)
        return fw, fe

    def yfaces(get):
        own, across = [], []
        for a in range(P_SIZE):
            s = t = None
            for p in range(PAIRS):
                v = get(a, p)
                s = gcoef[p] * v if s is None else s + gcoef[p] * v
                t = gcoef[PAIRS + p] * v if t is None else t + gcoef[PAIRS + p] * v
            u = halves(s, t) + srl(halves(t, s), 4)
            q = srl(u, 4)
            own.append(u)
            across.append(halves(lrl(q, 1), lrl(q, 127)))
        return own, across

    def send_halo(slot, get):
        fw, fe = xfaces(get)
        cw, ce = fw[0], srl(fe[0], -3)
        for p in range(1, PAIRS):
            cw = jnp.where(xpos == p, srl(fw[p], p), cw)
            ce = jnp.where(xpos == p, srl(fe[p], p - 3), ce)
        hsend[slot, 0] = cw
        hsend[slot, 1] = ce
        copies = [halo_copy(slot, 0, 0, west), halo_copy(slot, 1, 1, east)]
        for copy in copies:
            copy.start()
        own, across = yfaces(get)
        packed = across[0]
        for a in range(1, P_SIZE):
            mask = lane == jnp.where(low, a, a - 1)
            packed = jnp.where(mask, lrl(across[a], a), packed)
        hsend[slot, 2] = packed
        more = [halo_copy(slot, 2, 2, north), halo_copy(slot, 2, 3, south)]
        for copy in more:
            copy.start()
        return copies + more, (fw, fe, own, across)

    def halo_copy(slot, source, target, device):
        return pltpu.make_async_remote_copy(
            src_ref=hsend.at[slot, source],
            dst_ref=hrecv.at[slot, target],
            send_sem=hs_sem.at[slot, target],
            recv_sem=hr_sem.at[slot, target],
            device_id=device,
            device_id_type=MESH,
        )

    def take_halo(slot, copies):
        for copy in copies:
            copy.wait_recv()
        return (
            hrecv[slot, 0],
            hrecv[slot, 1],
            halves(hrecv[slot, 2], hrecv[slot, 3]),
        )

    edge = lane == jnp.where(low, 0, 127)

    def operate(get, halo, faces, emit):
        fw, fe, own, across = faces
        cw, ce, cy = halo
        stiff, open_w, open_e, open_y = small[0], small[1], small[2], small[3]
        sides = {}
        for p in range(PAIRS):
            nb_e = jnp.where(xpos == 3, srl(cw, 3 - p), srl(fw[p], 7))
            nb_w = jnp.where(xpos == 0, srl(ce, -p), srl(fe[p], 1))
            sides[0, p] = fw[p] - open_w * nb_w
            sides[P_SIZE - 1, p] = fe[p] - open_e * nb_e
        for a in range(P_SIZE):
            nb = jnp.where(edge, lrl(cy, -a), across[a])
            term = own[a] - open_y * nb
            vs = [get(a, p) for p in range(PAIRS)]
            ss = [srl(v, 4) for v in vs]
            for p in range(PAIRS):
                acc = None
                for r in range(PAIRS):
                    k = (p * PAIRS + r) * 2
                    part = coef[k] * vs[r] + coef[k + 1] * ss[r]
                    acc = part if acc is None else acc + part
                other = None
                for c in range(P_SIZE):
                    part = line[a, c] * get(c, p)
                    other = part if other is None else other + part
                value = tile(rea, a, p) * vs[p] + stiff * (acc + other)
                if p == 0:
                    value = value + jnp.where(low, term, 0.0)
                if p == PAIRS - 1:
                    value = value + jnp.where(low, 0.0, term)
                if (a, p) in sides:
                    value = value + sides[a, p]
                emit(a, p, value)

    def faces_of(get):
        fw, fe = xfaces(get)
        own, across = yfaces(get)
        return fw, fe, own, across

    def gather_rows(accs):
        zero = jnp.zeros((8, 128), jnp.float32)
        level = list(accs) + [zero] * (8 - len(accs))
        for shift in (1, 2, 4):
            keep = (sub // shift) % 2 == 0
            level = [
                jnp.where(keep, level[i], level[i + 1])
                + srl(jnp.where(keep, level[i + 1], level[i]), shift)
                for i in range(0, len(level), 2)
            ]
        return level[0]

    def fold(v):
        for shift in (4, 2, 1):
            v = v + srl(v, shift)
        return v

    def row_copy(slot, k):
        return pltpu.make_async_remote_copy(
            src_ref=rsend.at[slot],
            dst_ref=rrecv.at[slot, pl.ds(me, 1)],
            send_sem=rs_sem.at[slot],
            recv_sem=rr_sem.at[slot],
            device_id=peer(k),
            device_id_type=MESH,
        )

    def start_reduce(slot, accs):
        packed = None
        for start in range(0, len(accs), 8):
            sums = jnp.sum(gather_rows(accs[start:start + 8]), axis=1, keepdims=True)
            part = jnp.where(lane == sub + start, sums, 0.0)
            packed = part if packed is None else packed + part
        row = fold(packed)[0:1]
        rsend[slot] = row
        rrecv[slot, pl.ds(me, 1)] = row

        def push(k, carry):
            row_copy(slot, k).start()
            return carry

        lax.fori_loop(1, n, push, 0, unroll=n <= 64)

    def end_reduce(slot, count):
        block = rrecv.at[slot, pl.ds(0, n - 1)]
        pltpu.make_async_copy(block, block, rr_sem.at[slot]).wait()
        value = rrecv[slot, 0:8]
        for g in range(1, n // 8):
            value = value + rrecv[slot, 8 * g:8 * g + 8]
        value = fold(value)
        return [jnp.broadcast_to(value[:, k:k + 1], (8, 128)) for k in range(count)]

    get_ini = functools.partial(tile, ini)
    get_pend = functools.partial(tile, pend)
    get_image = functools.partial(tile, image)

    pl.semaphore_wait(barrier, n - 1)
    started = []
    copies, faces = send_halo(0, get_ini)
    started += copies
    halo = take_halo(0, copies)
    operate(get_ini, halo, faces, lambda a, p, v: put(pend, a, p, tile(src, a, p) - v))

    copies, faces = send_halo(1, get_pend)
    started += copies
    halo = take_halo(1, copies)

    hess = jnp.zeros((8, 128), jnp.float32)
    halos, written = [], []
    gram = {}
    for step in range(ITERS):
        last = step == ITERS - 1
        operate(get_pend, halo, faces, functools.partial(put, image))
        if not last:
            copies, _ = send_halo(step + 2, get_image)
            started += copies
        accs = [None] * (2 * step + 2 + (1 if last else 0))
        for a in range(P_SIZE):
            for p in range(PAIRS):
                w, v = get_image(a, p), get_pend(a, p)
                terms = [w * v, v * v]
                for i in range(step):
                    b = bas[i, pl.ds((a * PAIRS + p) * 8, 8), :]
                    terms += [b * w, b * v]
                if last:
                    terms.append(w * w)
                accs = [t if s is None else s + t for s, t in zip(accs, terms)]
        start_reduce(step, accs)
        sums = end_reduce(step, len(accs))
        beta = jnp.sqrt(sums[1] / total + FLOOR)
        inv = 1.0 / beta
        scaled = inv / total
        coeffs = [sums[2 + 2 * i] * scaled for i in range(step)] + [sums[0] * scaled * inv]
        for i in range(step):
            gram[i, step] = sums[3 + 2 * i] * scaled
        gram[step, step] = sums[1] * scaled * inv
        for i in range(step + 1):
            hess = jnp.where((sub == i) & (lane == step), coeffs[i], hess)
        if step:
            hess = jnp.where((sub == step) & (lane == step - 1), beta, hess)
        if last:
            square = sums[-1] * scaled * inv
            for i in range(ITERS):
                inner = None
                for k in range(ITERS):
                    g = gram[min(i, k), max(i, k)] * coeffs[k]
                    inner = g if inner is None else inner + g
                square = square + coeffs[i] * (inner - 2.0 * coeffs[i])
            final = jnp.sqrt(jnp.maximum(square, 0.0) + FLOOR)
            hess = jnp.where((sub == ITERS) & (lane == ITERS - 1), final, hess)
            post = 1.0 / final
        for a in range(P_SIZE):
            for p in range(PAIRS):
                b = get_pend(a, p) * inv
                bas[step, pl.ds((a * PAIRS + p) * 8, 8), :] = b
                v = get_image(a, p) * inv - coeffs[step] * b
                for i in range(step):
                    v = v - coeffs[i] * bas[i, pl.ds((a * PAIRS + p) * 8, 8), :]
                if last:
                    bas[ITERS, pl.ds((a * PAIRS + p) * 8, 8), :] = v * post
                else:
                    put(pend, a, p, v)
        out = pltpu.make_async_copy(bas.at[step], basis_out.at[step], out_sem.at[step])
        out.start()
        written.append(out)
        if not last:
            halos.append([h * inv for h in halo])
            fresh = take_halo(step + 2, copies)
            nxt = []
            for k in range(3):
                h = fresh[k] * inv
                for i in range(step + 1):
                    h = h - coeffs[i] * halos[i][k]
                nxt.append(h)
            halo = nxt
            faces = faces_of(get_pend)
    out = pltpu.make_async_copy(bas.at[ITERS], basis_out.at[ITERS], out_sem.at[ITERS])
    out.start()
    hess_out[...] = hess[0:ITERS + 1, 0:ITERS]
    for copy in started:
        copy.wait_send()
    for slot in range(ITERS):
        block = rrecv.at[slot, pl.ds(0, n - 1)]
        pltpu.make_async_copy(block, block, rs_sem.at[slot]).wait()
    for copy in written + [out]:
        copy.wait()


def body(nx, ny, source, initial, reaction, stiffness, line_op, face_deriv, wall_flags):
    nodes, ex, ey = source.shape
    n = nx * ny
    rows = nodes * ex
    flat = (rows, ey)
    total = float(nodes * ex * nx * ey * ny)
    vmem = pl.BlockSpec(memory_space=pltpu.VMEM)
    smem = pl.BlockSpec(memory_space=pltpu.SMEM)
    hess, basis = pl.pallas_call(
        functools.partial(kernel, nx, ny, total),
        out_shape=(
            jax.ShapeDtypeStruct((ITERS + 1, ITERS), jnp.float32),
            jax.ShapeDtypeStruct((ITERS + 1,) + flat, jnp.float32),
        ),
        in_specs=[smem, smem, vmem, vmem, vmem, vmem, vmem],
        out_specs=(vmem, pl.BlockSpec(memory_space=pl.ANY)),
        scratch_shapes=[
            pltpu.VMEM(flat, jnp.float32),
            pltpu.VMEM(flat, jnp.float32),
            pltpu.VMEM((ITERS + 1,) + flat, jnp.float32),
            pltpu.VMEM((2 * PAIRS * PAIRS, 8, 128), jnp.float32),
            pltpu.VMEM((2 * PAIRS, 8, 128), jnp.float32),
            pltpu.VMEM((4, 8, 128), jnp.float32),
            pltpu.VMEM((ITERS + 1, 3, 8, 128), jnp.float32),
            pltpu.VMEM((ITERS + 1, 4, 8, 128), jnp.float32),
            pltpu.VMEM((ITERS, 1, 128), jnp.float32),
            pltpu.VMEM((ITERS, n, 128), jnp.float32),
            pltpu.SemaphoreType.DMA((ITERS + 1, 4)),
            pltpu.SemaphoreType.DMA((ITERS + 1, 4)),
            pltpu.SemaphoreType.DMA((ITERS,)),
            pltpu.SemaphoreType.DMA((ITERS,)),
            pltpu.SemaphoreType.DMA((ITERS + 1,)),
        ],
        compiler_params=pltpu.CompilerParams(collective_id=0, has_side_effects=True),
    )(
        line_op, face_deriv, source.reshape(flat), initial.reshape(flat), reaction.reshape(flat),
        stiffness, wall_flags,
    )
    return hess, basis.reshape((ITERS + 1, nodes, ex, ey))


def solution(mesh):
    return jax.shard_map(
        functools.partial(body, mesh.shape["gx"], mesh.shape["gy"]),
        mesh=mesh,
        in_specs=(
            P(None, "gx", "gy"),
            P(None, "gx", "gy"),
            P(None, "gx", "gy"),
            P("gx", "gy"),
            P(),
            P(),
            P(None, "gx", "gy"),
        ),
        out_specs=(P(), P(None, None, "gx", "gy")),
        check_vma=False,
    )
```

time: 410 us -> 45.9 us (0.11)
  blocking collectives: 236 us -> 0 us
  waiting for transfers between devices: 61.2 us -> 0 us
  Pallas kernels: 0 us -> 41.8 us
  matrix products: 36.9 us -> 0 us
  starting transfers between devices: 35.6 us -> 0 us
  other arithmetic: 13.3 us -> 0 us
  local copies, waits for them, and re-layouts: 15.6 us -> 3.32 us
  loops' own time: 7.86 us -> 0 us
    psum x6 -> x0, blocking collectives: 236 us -> none  [the longest x5 196 us: advance(): lax.psum((local, local_total(pending * image), local_total(pending * pend...]
    ppermute x24 -> x0, waiting for transfers between devices: 61.2 us -> none  [the longest x12 34.7 us: extended(): before = lax.ppermute(last, axis, up)]
    pallas_call x0 -> x1, Pallas kernels: none -> 41.8 us  [body(): pl.pallas_call(functools.partial(kernel, nx, ny, total), out_shape=(jax.S...]
    dot_general x46 -> x0, matrix products: 36.9 us -> none  [the longest x5 13 us: products(): per_cell = jnp.einsum('kqxy,qxy->kxy', basis, image, precision=highest)]
    ppermute x24 -> x0, starting transfers between devices: 35.6 us -> none  [the longest x12 32.4 us: extended(): after = lax.ppermute(leading, axis, down)]
    reduce_sum x12 -> x0, other arithmetic: 8.74 us -> none  [local_total(): return jnp.sum(jnp.sum(values, axis=0))]
    another operation x1 -> x0, loops' own time: 7.86 us -> none  [body(): lax.fori_loop(0, ITERS, advance, (basis, hessen, first))]
  transfers between devices with their start and end apart: 24 -> 0, of which waited for: 23 -> 0; matrix products, arithmetic and copies ran while one was open for 1% -> 0% of each run, Pallas kernels for 0% -> 0%
where the time goes in v1:
time: 45.9 us; the launch traced here: 45.7 us
  Pallas kernels  41.8 us (91%)
  local copies, waits for them, and re-layouts  3.32 us (7%)
  between operations  0.65 us (1%)
    pallas_call x1, Pallas kernels, body(): pl.pallas_call(functools.partial(kernel, nx, ny, total), out_shape=(jax.S...  41.8 us
    unnamed x4, local copies, waits for them, and re-layouts  3.32 us

profile of v1, /device:TPU:0, one launch (start us, length us, event | category | flops | bytes accessed | tf_op | source)
XLA Modules:
  0.0 45.7 jit_solution(16525824515523854860)
XLA Ops:
  0.6 41.8 %shard_map.86 = (f32[6,5]{1,0:T(8,128)}, f32[6,256,128]{2,1,0:T(8,128)}) custom-call(f32[8,8]{1,0:T(8,128)} %line.1, f32[8]{0:T(128)} %deriv.1, f32[256,128]{1,0:T(8,128)} %bitcast.5, f32[256,128]{1,0:T(8,128)} %bitcast.6, f32[256,128]{1,0:T(8,128)} %bitcast.7, f32[4,128]{1,0:T(4,128)} %stf.1, s32[4,4,128]{2,1,0:T(4,128)} %wal.1), custom_call_target="tpu_custom_call" | custom-call | tf_op jit(solution)/shard_map/pallas_call | solution.py:351
  42.4 0.0 copy-start
  42.4 0.7 %copy-done = f32[6,5]{1,0:T(8,128)S(1)} copy-done((f32[6,5]{1,0:T(8,128)S(1)}, f32[6,5]{1,0:T(8,128)}, u32[]{:S(2)}) %copy-start) | copy-done | bytes 144
  43.1 0.6 %copy.11 = f32[6,5]{1,0:T(8,128)} copy(f32[6,5]{1,0:T(8,128)S(1)} %copy-done) | data formatting | bytes 240
  43.7 2.1 %copy.12 = f32[6,64,4,128]{3,2,1,0:T(4,128)} copy(f32[6,64,4,128]{3,2,1,0:T(4,128)} %bitcast.4) | data formatting | bytes 1572864
Async XLA Ops:
  42.4 0.7 %copy-start = (f32[6,5]{1,0:T(8,128)S(1)}, f32[6,5]{1,0:T(8,128)}, u32[]{:S(2)}) copy-start(f32[6,5]{1,0:T(8,128)} %get-tuple-element.8) | copy-start | bytes 364

commit v2 on v1

--- a/solution.py
+++ b/solution.py
@@ -17,19 +17,34 @@
 
 def kernel(
     nx, ny, total,
-    line, deriv, src, ini, rea, stf, wal,
-    hess_out, basis_out,
-    pend, image, bas, coef, gcoef, small,
+    line, deriv, src_any, ini_any, rea_any, stf, wal,
+    hess_out, bas,
+    pend, image, coef, gcoef, small, src, ini, rea, in_sem,
     hsend, hrecv, rsend, rrecv,
-    hs_sem, hr_sem, rs_sem, rr_sem, out_sem,
+    hs_sem, hr_sem, rs_sem, rr_sem,
 ):
     n = nx * ny
     gx, gy = lax.axis_index("gx"), lax.axis_index("gy")
     me = gx * ny + gy
 
-    def peer(k):
-        t = lax.rem(me + k, n)
-        return (t // ny, lax.rem(t, ny))
+    side = gy // (ny // 2)
+    offsets = sorted(range(1, nx), key=lambda d: abs(2 * d - nx))
+
+    def for_peers(act):
+        def column(k, own_column):
+            across = side * k + (1 - side) * (ny - 1 - k)
+            for d in offsets:
+                act((lax.rem(gx + d, nx), across))
+            if own_column:
+                skip = jnp.where(k >= (side * gy + (1 - side) * (ny - 1 - gy)), 1, 0)
+                act((gx, across + (2 * side - 1) * skip))
+
+        if n <= 64:
+            for k in range(ny - 1):
+                column(k, True)
+        else:
+            lax.fori_loop(0, ny - 1, lambda k, c: (column(k, True), c)[1], 0)
+        column(ny - 1, False)
 
     east = (lax.rem(gx + 1, nx), gy)
     west = (lax.rem(gx + nx - 1, nx), gy)
@@ -38,11 +53,16 @@
 
     barrier = pltpu.get_barrier_semaphore()
 
-    def greet(k, carry):
-        pl.semaphore_signal(barrier, inc=1, device_id=peer(k), device_id_type=MESH)
-        return carry
-
-    lax.fori_loop(1, n, greet, 0, unroll=n <= 64)
+    def greet(device):
+        pl.semaphore_signal(barrier, inc=1, device_id=device, device_id_type=MESH)
+
+    loads = [
+        pltpu.make_async_copy(given, held, in_sem.at[k])
+        for k, (given, held) in enumerate(((ini_any, ini), (src_any, src), (rea_any, rea)))
+    ]
+    for load in loads:
+        load.start()
+    for_peers(greet)
 
     sub = lax.broadcasted_iota(jnp.int32, (8, 128), 0)
     lane = lax.broadcasted_iota(jnp.int32, (8, 128), 1)
@@ -110,7 +130,7 @@
             across.append(halves(lrl(q, 1), lrl(q, 127)))
         return own, across
 
-    def send_halo(slot, get):
+    def send_halo(slot, get, ready=lambda: None):
         fw, fe = xfaces(get)
         cw, ce = fw[0], srl(fe[0], -3)
         for p in range(1, PAIRS):
@@ -118,19 +138,20 @@
             ce = jnp.where(xpos == p, srl(fe[p], p - 3), ce)
         hsend[slot, 0] = cw
         hsend[slot, 1] = ce
-        copies = [halo_copy(slot, 0, 0, west), halo_copy(slot, 1, 1, east)]
-        for copy in copies:
-            copy.start()
         own, across = yfaces(get)
         packed = across[0]
         for a in range(1, P_SIZE):
             mask = lane == jnp.where(low, a, a - 1)
             packed = jnp.where(mask, lrl(across[a], a), packed)
         hsend[slot, 2] = packed
-        more = [halo_copy(slot, 2, 2, north), halo_copy(slot, 2, 3, south)]
-        for copy in more:
+        ready()
+        copies = [
+            halo_copy(slot, 2, 2, north), halo_copy(slot, 2, 3, south),
+            halo_copy(slot, 0, 0, west), halo_copy(slot, 1, 1, east),
+        ]
+        for copy in copies:
             copy.start()
-        return copies + more, (fw, fe, own, across)
+        return copies, (fw, fe, own, across)
 
     def halo_copy(slot, source, target, device):
         return pltpu.make_async_remote_copy(
@@ -209,13 +230,13 @@
             v = v + srl(v, shift)
         return v
 
-    def row_copy(slot, k):
+    def row_copy(slot, device):
         return pltpu.make_async_remote_copy(
             src_ref=rsend.at[slot],
             dst_ref=rrecv.at[slot, pl.ds(me, 1)],
             send_sem=rs_sem.at[slot],
             recv_sem=rr_sem.at[slot],
-            device_id=peer(k),
+            device_id=device,
             device_id_type=MESH,
         )
 
@@ -229,11 +250,7 @@
         rsend[slot] = row
         rrecv[slot, pl.ds(me, 1)] = row
 
-        def push(k, carry):
-            row_copy(slot, k).start()
-            return carry
-
-        lax.fori_loop(1, n, push, 0, unroll=n <= 64)
+        for_peers(lambda device: row_copy(slot, device).start())
 
     def end_reduce(slot, count):
         block = rrecv.at[slot, pl.ds(0, n - 1)]
@@ -248,9 +265,11 @@
     get_pend = functools.partial(tile, pend)
     get_image = functools.partial(tile, image)
 
-    pl.semaphore_wait(barrier, n - 1)
     started = []
-    copies, faces = send_halo(0, get_ini)
+    loads[0].wait()
+    copies, faces = send_halo(0, get_ini, lambda: pl.semaphore_wait(barrier, n - 1))
+    loads[1].wait()
+    loads[2].wait()
     started += copies
     halo = take_halo(0, copies)
     operate(get_ini, halo, faces, lambda a, p, v: put(pend, a, p, tile(src, a, p) - v))
@@ -260,7 +279,7 @@
     halo = take_halo(1, copies)
 
     hess = jnp.zeros((8, 128), jnp.float32)
-    halos, written = [], []
+    halos = []
     gram = {}
     for step in range(ITERS):
         last = step == ITERS - 1
@@ -314,9 +333,6 @@
                     bas[ITERS, pl.ds((a * PAIRS + p) * 8, 8), :] = v * post
                 else:
                     put(pend, a, p, v)
-        out = pltpu.make_async_copy(bas.at[step], basis_out.at[step], out_sem.at[step])
-        out.start()
-        written.append(out)
         if not last:
             halos.append([h * inv for h in halo])
             fresh = take_halo(step + 2, copies)
@@ -328,15 +344,22 @@
                 nxt.append(h)
             halo = nxt
             faces = faces_of(get_pend)
-    out = pltpu.make_async_copy(bas.at[ITERS], basis_out.at[ITERS], out_sem.at[ITERS])
-    out.start()
     hess_out[...] = hess[0:ITERS + 1, 0:ITERS]
     for copy in started:
         copy.wait_send()
     for slot in range(ITERS):
         block = rrecv.at[slot, pl.ds(0, n - 1)]
         pltpu.make_async_copy(block, block, rs_sem.at[slot]).wait()
-    for copy in written + [out]:
+
+
+def store(hess, basis, hess_out, basis_out, sem):
+    copies = [
+        pltpu.make_async_copy(basis, basis_out, sem.at[0]),
+        pltpu.make_async_copy(hess, hess_out, sem.at[1]),
+    ]
+    for copy in copies:
+        copy.start()
+    for copy in copies:
         copy.wait()
 
 
@@ -347,22 +370,26 @@
     flat = (rows, ey)
     total = float(nodes * ex * nx * ey * ny)
     vmem = pl.BlockSpec(memory_space=pltpu.VMEM)
+    hbm = pl.BlockSpec(memory_space=pl.ANY)
     smem = pl.BlockSpec(memory_space=pltpu.SMEM)
     hess, basis = pl.pallas_call(
         functools.partial(kernel, nx, ny, total),
         out_shape=(
-            jax.ShapeDtypeStruct((ITERS + 1, ITERS), jnp.float32),
-            jax.ShapeDtypeStruct((ITERS + 1,) + flat, jnp.float32),
+            pltpu.VMEM((ITERS + 1, ITERS), jnp.float32),
+            pltpu.VMEM((ITERS + 1,) + flat, jnp.float32),
         ),
-        in_specs=[smem, smem, vmem, vmem, vmem, vmem, vmem],
-        out_specs=(vmem, pl.BlockSpec(memory_space=pl.ANY)),
+        in_specs=[smem, smem, hbm, hbm, hbm, vmem, vmem],
+        out_specs=(vmem, vmem),
         scratch_shapes=[
             pltpu.VMEM(flat, jnp.float32),
             pltpu.VMEM(flat, jnp.float32),
-            pltpu.VMEM((ITERS + 1,) + flat, jnp.float32),
             pltpu.VMEM((2 * PAIRS * PAIRS, 8, 128), jnp.float32),
             pltpu.VMEM((2 * PAIRS, 8, 128), jnp.float32),
             pltpu.VMEM((4, 8, 128), jnp.float32),
+            pltpu.VMEM(flat, jnp.float32),
+            pltpu.VMEM(flat, jnp.float32),
+            pltpu.VMEM(flat, jnp.float32),
+            pltpu.SemaphoreType.DMA((3,)),
             pltpu.VMEM((ITERS + 1, 3, 8, 128), jnp.float32),
             pltpu.VMEM((ITERS + 1, 4, 8, 128), jnp.float32),
             pltpu.VMEM((ITERS, 1, 128), jnp.float32),
@@ -371,13 +398,24 @@
             pltpu.SemaphoreType.DMA((ITERS + 1, 4)),
             pltpu.SemaphoreType.DMA((ITERS,)),
             pltpu.SemaphoreType.DMA((ITERS,)),
-            pltpu.SemaphoreType.DMA((ITERS + 1,)),
         ],
         compiler_params=pltpu.CompilerParams(collective_id=0, has_side_effects=True),
     )(
         line_op, face_deriv, source.reshape(flat), initial.reshape(flat), reaction.reshape(flat),
         stiffness, wall_flags,
     )
+    hess = pltpu.with_memory_space_constraint(hess, pltpu.VMEM)
+    basis = pltpu.with_memory_space_constraint(basis, pltpu.VMEM)
+    hess, basis = pl.pallas_call(
+        store,
+        out_shape=(
+            jax.ShapeDtypeStruct(hess.shape, jnp.float32),
+            jax.ShapeDtypeStruct(basis.shape, jnp.float32),
+        ),
+        in_specs=[hbm, hbm],
+        out_specs=(hbm, hbm),
+        scratch_shapes=[pltpu.SemaphoreType.DMA((2,))],
+    )(hess, basis)
     return hess, basis.reshape((ITERS + 1, nodes, ex, ey))
 
 

time: 45.9 us -> 41.6 us (0.906)
  local copies, waits for them, and re-layouts: 3.32 us -> 0 us
  Pallas kernels: 41.8 us -> 40.7 us
    unnamed x4 -> x0, local copies, waits for them, and re-layouts: 3.32 us -> none
    pallas_call x1 -> x2, Pallas kernels: 41.8 us -> 40.7 us  [the longest x1 39.8 us: body(): pl.pallas_call(functools.partial(kernel, nx, ny, total), out_shape=(pltpu...]
where the time goes in v2:
time: 41.6 us; the launch traced here: 41.4 us
  Pallas kernels  40.7 us (98%)
  between operations  0.64 us (2%)
    pallas_call x1, Pallas kernels, body(): pl.pallas_call(functools.partial(kernel, nx, ny, total), out_shape=(pltpu...  39.8 us
    pallas_call x1, Pallas kernels, body(): pl.pallas_call(store, out_shape=(jax.ShapeDtypeStruct(hess.shape, jnp.flo...  0.9 us

profile of v2, /device:TPU:0, one launch (start us, length us, event | category | flops | bytes accessed | tf_op | source)
XLA Modules:
  0.0 41.4 jit_solution(15844825048896558720)
XLA Ops:
  0.6 39.8 %shard_map.86 = (f32[6,5]{1,0:T(8,128)S(1)}, f32[6,256,128]{2,1,0:T(8,128)S(1)}) custom-call(f32[8,8]{1,0:T(8,128)} %line.1, f32[8]{0:T(128)} %deriv.1, f32[256,128]{1,0:T(8,128)} %bitcast.4, f32[256,128]{1,0:T(8,128)} %bitcast.5, f32[256,128]{1,0:T(8,128)} %bitcast.6, f32[4,128]{1,0:T(4,128)} %stf.1, s32[4,4,128]{2,1,0:T(4,128)} %wal.1), custom_call_target="tpu_custom_call" | custom-call | tf_op jit(solution)/shard_map/pallas_call | solution.py:375
  40.5 0.9 %shard_map.87 = (f32[6,5]{1,0:T(8,128)}, f32[6,256,128]{2,1,0:T(8,128)}) custom-call(f32[6,5]{1,0:T(8,128)S(1)} %get-tuple-element.6.hess, f32[6,256,128]{2,1,0:T(8,128)S(1)} %get-tuple-element.7.basis), custom_call_target="tpu_custom_call" | custom-call | tf_op jit(solution)/shard_map/pallas_call | solution.py:409
